TPU v7x, 32 devices: a whole 2x2x4 slice. The times are simulated.
32 devices in a mesh: docs: 8 (over z, x), rep: 4 (over y, core).
Axes of the slice: x: 2, y: 2, z: 4, core: 2. Of those that a mesh axis runs over, the one named last changes fastest.
Arguments:
- embeddings: bfloat16 [32768, 4096], P(('docs', 'rep')), may hold values from -6 to 6
- pca_basis: bfloat16 [4096, 256], replicated, may hold values from -0.09375 to 0.09375
- cluster: int32 [32768, 1], P(('docs', 'rep')), may hold values from 0 to 31; in each aligned block of 1024 rows (0 to 1023, 1024 to 2047, ...) at most 64 rows name the same one
- doc_index: int32 [32768], P(('docs', 'rep')), may hold values from 0 to 32767, each once
Outputs:
- nearest_sim: float32 [32768], P(('docs', 'rep'))
Inputs may be any that keep to these rules, and one draw needn't show every extreme that they name: In each device's block of 1024 rows no cluster is named by more than 64 rows, a bound that some block reaches. `doc_index`: each document number appears once.
All inputs are finite; a program needn't handle non-finite values.
Results may differ from a plain program's by a relative error of at most 0.0014.
Values may be sent and summed in bfloat16 or wider, within the bound.
No kernel may reach another device: no remote copies, remote signals or barrier semaphores. Data moves between devices by JAX's collectives and lax.ppermute only.
A program may use at most 64 MiB of HBM per device.

v0:
```python
import jax
import jax.numpy as jnp
from jax import lax
from jax.sharding import PartitionSpec as P

CL_DEV = 4


sentinel_index = 2**30


def on_device(embeddings, pca_basis, cluster, doc_index):
    n_docs = lax.axis_size("docs")
    n_rep = lax.axis_size("rep")
    doc_rows = embeddings.shape[0]
    features = pca_basis.shape[1]
    slot_depth = max(2, 2 * doc_rows // (CL_DEV * n_docs))
    clusters = CL_DEV * n_docs
    projected = jnp.dot(embeddings, pca_basis, preferred_element_type=jnp.float32)
    unit_rows = (
        projected * lax.rsqrt(jnp.sum(projected * projected, axis=1, keepdims=True) + 1e-06)
    ).astype(jnp.bfloat16)
    cluster_id = cluster[:, 0]
    one_hot = (cluster_id[:, None] == jnp.arange(clusters, dtype=jnp.int32)[None, :]).astype(
        jnp.bfloat16
    )
    positions = jnp.arange(doc_rows, dtype=jnp.int32)
    before = (positions[None, :] < positions[:, None]).astype(jnp.bfloat16)
    earlier = jnp.dot(before, one_hot, preferred_element_type=jnp.float32)
    member_rank = jnp.sum(earlier * one_hot.astype(jnp.float32), axis=1).astype(jnp.int32)
    slot_of = cluster_id * slot_depth + member_rank
    send_rows = (
        jnp.zeros((clusters * slot_depth, features), jnp.bfloat16).at[slot_of].set(unit_rows)
    )
    send_index = (
        jnp.full((clusters * slot_depth,), sentinel_index, jnp.int32).at[slot_of].set(doc_index)
    )
    per_rep = CL_DEV // n_rep
    recv_rows, recv_index = (
        lax.all_to_all(
            lax.all_to_all(
                send_rows.reshape(n_docs, n_rep, per_rep * slot_depth, features),
                "docs",
                split_axis=0,
                concat_axis=0,
                tiled=True,
            ),
            "rep",
            split_axis=1,
            concat_axis=1,
            tiled=True,
        ),
        lax.all_to_all(
            lax.all_to_all(
                send_index.reshape(n_docs, n_rep, per_rep * slot_depth),
                "docs",
                split_axis=0,
                concat_axis=0,
                tiled=True,
            ),
            "rep",
            split_axis=1,
            concat_axis=1,
            tiled=True,
        ),
    )
    member_rows = jnp.moveaxis(
        recv_rows.reshape(n_docs, n_rep, per_rep, slot_depth, features), 2, 0
    ).reshape(per_rep, -1, features)
    member_index = jnp.moveaxis(
        recv_index.reshape(n_docs, n_rep, per_rep, slot_depth), 2, 0
    ).reshape(per_rep, -1)

    def within(inputs):
        rows_here, index_here = inputs
        scores = jnp.einsum("ip,jp->ij", rows_here, rows_here, preferred_element_type=jnp.float32)
        allowed = index_here[None, :] < index_here[:, None]
        return jnp.max(jnp.where(allowed, scores, -1.0), axis=1)

    found = lax.map(within, (member_rows, member_index))
    found = jnp.moveaxis(found.reshape(per_rep, n_docs, n_rep, slot_depth), 0, 2).reshape(
        n_docs, n_rep, per_rep * slot_depth
    )
    returned = lax.all_to_all(
        lax.all_to_all(found, "docs", split_axis=0, concat_axis=0, tiled=True),
        "rep",
        split_axis=1,
        concat_axis=1,
        tiled=True,
    )
    nearest = returned.reshape(-1)[slot_of]
    return nearest


def solution(mesh):
    return jax.shard_map(
        on_device,
        mesh=mesh,
        in_specs=(P(("docs", "rep"), None), P(), P(("docs", "rep"), None), P(("docs", "rep"))),
        out_specs=P(("docs", "rep")),
        check_vma=False,
    )
```

profile of v0, /device:TPU:0, one launch (start us, length us, event | category | flops | bytes accessed | tf_op | source)
XLA Modules:
  0.0 116.1 jit_solution(2289692478517513636)
XLA Ops:
  0.0 0.0 copy-start
  0.0 1.4 %fusion.2 = f32[1024]{0:T(1024)S(1)} fusion(s32[1024]{0:T(1024)} %bitcast.27), kind=kOutput, calls=%fused_computation.7 | convolution fusion | flops 68353024 | bytes 8192 | tf_op jit(solution)/shard_map/dot_general | solution.py:29
  1.4 0.7 compare_select_fusion
  2.1 4.5 %scatter_custom_fusion = s32[2048]{0:T(1024)S(1)} fusion(s32[1024]{0:T(1024)S(1)} %bitcast.23, s32[1024]{0:T(1024)} %param.7, s32[]{:T(128)} %constant.9.clone.1), kind=kCustom, calls=%fused_computation.17 | custom fusion | bytes 8704 | tf_op jit(solution)/shard_map/scatter | solution.py:36
  6.6 0.1 reshape.29
  6.7 0.7 reshape.60
  7.4 7.3 %all-to-all-start = ((s32[8,1,256]{2,1,0:T(1,128)}), s32[8,1,256]{2,1,0:T(1,128)S(1)}, u32[]{:S(2)}, u32[]{:S(2)}) async-start(s32[8,1,256]{2,1,0:T(1,128)} %reshape.60), calls=%async_computation | async-start | bytes 16384 | tf_op jit(solution)/shard_map/all_to_all | solution.py:54
  14.6 0.0 copy-done
  14.6 5.8 %multiply_reduce_fusion = (f32[1024]{0:T(1024)S(1)}, f32[1024,256]{0,1:T(8,128)S(1)}) fusion(bf16[1024,4096]{1,0:T(8,128)(2,1)} %param.4, bf16[4096,256]{1,0:T(8,128)(2,1)S(1)} %copy-done), kind=kOutput, calls=%fused_computation.9 | convolution fusion | flops 2148006912 | bytes 11538432 | tf_op jit(solution)/shard_map/dot_general | solution.py:19
  20.4 0.1 multiply_convert_fusion
  20.5 0.2 copy.17
  20.7 6.0 %scatter_custom_fusion.1 = bf16[2048,256]{1,0:T(8,128)(2,1)} fusion(s32[1024]{0:T(1024)S(1)} %bitcast.24, bf16[1024,256]{1,0:T(8,128)(2,1)S(1)} %copy.17, bf16[]{:T(256)} %constant.14.clone.1), kind=kCustom, calls=%fused_computation.10 | custom fusion | bytes 1048578 | tf_op jit(solution)/shard_map/scatter | solution.py:33
  26.8 0.0 all-to-all-done
  26.8 6.0 %all-to-all-start.2 = ((bf16[8,4,64,256]{3,2,1,0:T(8,128)(2,1)}), bf16[8,4,64,256]{3,2,1,0:T(8,128)(2,1)S(1)}, u32[]{:S(2)}, u32[]{:S(2)}) async-start(bf16[8,4,64,256]{3,2,1,0:T(8,128)(2,1)} %bitcast.17), calls=%async_computation.2 | async-start | bytes 2097152 | tf_op jit(solution)/shard_map/all_to_all | solution.py:41
  32.8 0.5 broadcast.22
  33.3 0.7 reduce
  34.0 0.1 reshape.61
  34.0 0.7 reshape.62
  34.7 23.5 %all-to-all-done.2 = bf16[8,4,64,256]{3,2,1,0:T(8,128)(2,1)S(1)} async-done(((bf16[8,4,64,256]{3,2,1,0:T(8,128)(2,1)}), bf16[8,4,64,256]{3,2,1,0:T(8,128)(2,1)S(1)}, u32[]{:S(2)}, u32[]{:S(2)}) %all-to-all-start.2) | async-done | bytes 1048608 | tf_op jit(solution)/shard_map/all_to_all | solution.py:41
  58.2 3.2 %all-to-all-start.1 = ((s32[4,1,512]{2,1,0:T(1,128)}), s32[4,1,512]{2,1,0:T(1,128)S(1)}, u32[]{:S(2)}, u32[]{:S(2)}) async-start(s32[4,1,512]{2,1,0:T(1,128)} %reshape.62), calls=%async_computation.1 | async-start | bytes 16384 | tf_op jit(solution)/shard_map/all_to_all | solution.py:53
  61.5 1.1 copy.18
  62.5 2.7 %all-to-all-done.1 = s32[4,1,512]{2,1,0:T(1,128)S(1)} async-done(((s32[4,1,512]{2,1,0:T(1,128)}), s32[4,1,512]{2,1,0:T(1,128)S(1)}, u32[]{:S(2)}, u32[]{:S(2)}) %all-to-all-start.1) | async-done | bytes 8224 | tf_op jit(solution)/shard_map/all_to_all | solution.py:53
  65.2 3.5 %all-to-all-start.3 = ((bf16[8,4,64,256]{3,2,0,1:T(8,128)(2,1)}), bf16[8,4,64,256]{3,2,0,1:T(8,128)(2,1)S(1)}, u32[]{:S(2)}, u32[]{:S(2)}) async-start(bf16[8,4,64,256]{3,2,0,1:T(8,128)(2,1)} %copy.18), calls=%async_computation.3 | async-start | bytes 2097152 | tf_op jit(solution)/shard_map/all_to_all | solution.py:40
  68.8 0.7 reduce.1
  69.4 0.1 reshape.63
  69.5 0.1 lt.46
  69.6 13.6 %all-to-all-done.3 = bf16[8,4,64,256]{3,2,0,1:T(8,128)(2,1)S(1)} async-done(((bf16[8,4,64,256]{3,2,0,1:T(8,128)(2,1)}), bf16[8,4,64,256]{3,2,0,1:T(8,128)(2,1)S(1)}, u32[]{:S(2)}, u32[]{:S(2)}) %all-to-all-start.3) | async-done | bytes 1048608 | tf_op jit(solution)/shard_map/all_to_all | solution.py:40
  83.2 0.1 copy.19
  83.2 2.6 %select_reduce_fusion = f32[2048]{0:T(1024)S(1)} fusion(bf16[2048,256]{1,0:T(8,128)(2,1)S(1)} %bitcast.18, s32[2048]{0:T(1024)S(1)} %lt.46), kind=kOutput, calls=%fused_computation.3 | convolution fusion | flops 2160064512 | bytes 1064960 | tf_op jit(solution)/shard_map/while/body/eval_jaxpr/ip,jp->ij/dot_general | solution.py:76
  85.9 0.1 reshape_transpose_reshape.2
  85.9 0.1 reshape.64
  86.0 9.7 %all_to_all.30 = f32[8,1,256]{2,1,0:T(1,128)S(1)} all-to-all(f32[8,1,256]{2,1,0:T(1,128)S(1)} %reshape.64), channel_id=1, replica_groups=mesh['docs'=8,'rep'=4] {'docs'}, dimensions={0} | all-to-all | bytes 16384 | tf_op jit(solution)/shard_map/all_to_all | solution.py:85
  95.7 0.5 broadcast.24
  96.2 0.7 reduce.2
  96.9 0.1 reshape.65
  97.0 0.7 reshape.66
  97.7 3.2 %all-to-all-start.5 = ((f32[4,1,512]{2,1,0:T(1,128)}), f32[4,1,512]{2,1,0:T(1,128)S(1)}, u32[]{:S(2)}, u32[]{:S(2)}) async-start(f32[4,1,512]{2,1,0:T(1,128)} %reshape.66), calls=%async_computation.5 | async-start | bytes 16384 | tf_op jit(solution)/shard_map/all_to_all | solution.py:84
  100.9 3.8 %all-to-all-done.5 = f32[4,1,512]{2,1,0:T(1,128)S(1)} async-done(((f32[4,1,512]{2,1,0:T(1,128)}), f32[4,1,512]{2,1,0:T(1,128)S(1)}, u32[]{:S(2)}, u32[]{:S(2)}) %all-to-all-start.5) | async-done | bytes 8224 | tf_op jit(solution)/shard_map/all_to_all | solution.py:84
  104.7 0.7 reduce.3
  105.4 0.1 reshape.67
  105.5 0.1 reshape.31
  105.5 10.5 %gather_fusion = f32[1024]{0:T(1024)} fusion(f32[2048]{0:T(1024)S(1)} %reshape.31, s32[1024]{0:T(1024)S(1)} %broadcast_clamp_fusion), kind=kCustom, calls=%fused_computation | custom fusion | bytes 12288 | tf_op jit(solution)/shard_map/gather | solution.py:91
  (7 shorter events, 0.0 us)
Async XLA Ops:
  0.0 14.6 %copy-start = (bf16[4096,256]{1,0:T(8,128)(2,1)S(1)}, bf16[4096,256]{1,0:T(8,128)(2,1)}, u32[]{:S(2)}) copy-start(bf16[4096,256]{1,0:T(8,128)(2,1)} %param.5) | copy-start | bytes 6291460
  7.4 19.4 %all-to-all-start = ((s32[8,1,256]{2,1,0:T(1,128)}), s32[8,1,256]{2,1,0:T(1,128)S(1)}, u32[]{:S(2)}, u32[]{:S(2)}) async-start(s32[8,1,256]{2,1,0:T(1,128)} %reshape.60), calls=%async_computation | async-start | bytes 16384 | tf_op jit(solution)/shard_map/all_to_all | solution.py:54
  26.8 31.4 %all-to-all-start.2 = ((bf16[8,4,64,256]{3,2,1,0:T(8,128)(2,1)}), bf16[8,4,64,256]{3,2,1,0:T(8,128)(2,1)S(1)}, u32[]{:S(2)}, u32[]{:S(2)}) async-start(bf16[8,4,64,256]{3,2,1,0:T(8,128)(2,1)} %bitcast.17), calls=%async_computation.2 | async-start | bytes 2097152 | tf_op jit(solution)/shard_map/all_to_all | solution.py:41
  58.2 7.0 %all-to-all-start.1 = ((s32[4,1,512]{2,1,0:T(1,128)}), s32[4,1,512]{2,1,0:T(1,128)S(1)}, u32[]{:S(2)}, u32[]{:S(2)}) async-start(s32[4,1,512]{2,1,0:T(1,128)} %reshape.62), calls=%async_computation.1 | async-start | bytes 16384 | tf_op jit(solution)/shard_map/all_to_all | solution.py:53
  65.2 17.9 %all-to-all-start.3 = ((bf16[8,4,64,256]{3,2,0,1:T(8,128)(2,1)}), bf16[8,4,64,256]{3,2,0,1:T(8,128)(2,1)S(1)}, u32[]{:S(2)}, u32[]{:S(2)}) async-start(bf16[8,4,64,256]{3,2,0,1:T(8,128)(2,1)} %copy.18), calls=%async_computation.3 | async-start | bytes 2097152 | tf_op jit(solution)/shard_map/all_to_all | solution.py:40
  97.7 7.0 %all-to-all-start.5 = ((f32[4,1,512]{2,1,0:T(1,128)}), f32[4,1,512]{2,1,0:T(1,128)S(1)}, u32[]{:S(2)}, u32[]{:S(2)}) async-start(f32[4,1,512]{2,1,0:T(1,128)} %reshape.66), calls=%async_computation.5 | async-start | bytes 16384 | tf_op jit(solution)/shard_map/all_to_all | solution.py:84
where the time goes:
time: 117 us; the launch traced here: 116 us
  waiting for transfers between devices  43.5 us (37%)
  local copies, waits for them, and re-layouts  26.2 us (22%)
  starting transfers between devices  23.3 us (20%)
  matrix products  9.78 us (8%)
  blocking collectives  9.68 us (8%)
  other arithmetic  3.5 us (3%)
    all_to_all x1, waiting for transfers between devices, on_device(): lax.all_to_all(send_rows.reshape(n_docs, n_rep, per_rep * slot_depth, fea...  23.5 us
    all_to_all x1, waiting for transfers between devices, on_device(): lax.all_to_all(lax.all_to_all(send_rows.reshape(n_docs, n_rep, per_rep *...  13.6 us
    gather x1, local copies, waits for them, and re-layouts, on_device(): nearest = returned.reshape(-1)[slot_of]  10.5 us
    all_to_all x1, blocking collectives, on_device(): lax.all_to_all(found, 'docs', split_axis=0, concat_axis=0, tiled=True)  9.68 us
    all_to_all x1, starting transfers between devices, on_device(): lax.all_to_all(send_index.reshape(n_docs, n_rep, per_rep * slot_depth), '...  7.28 us
    scatter x1, local copies, waits for them, and re-layouts, on_device(): jnp.zeros((clusters * slot_depth, features), jnp.bfloat16).at[slot_of]  6.03 us
    all_to_all x1, starting transfers between devices, on_device(): lax.all_to_all(send_rows.reshape(n_docs, n_rep, per_rep * slot_depth, fea...  5.99 us
    dot_general x1, matrix products, on_device(): jnp.dot(embeddings, pca_basis, preferred_element_type=jnp.float32)  5.76 us
  transfers between devices with their start and end apart: 5, of which 4 were waited for; matrix products, arithmetic and copies ran while one was open for 14% of the time, Pallas kernels for 0%

commit v1 on v0

v1 whole, which is shorter than its diff:
```python
import jax
import jax.numpy as jnp
from jax import lax
from jax.experimental import pallas as pl
from jax.experimental.pallas import tpu as pltpu
from jax.sharding import PartitionSpec as P

CL_DEV = 4
AXES = ("docs", "rep")
LANES = 128
EXTRA = 8
CHUNKS = 8
BASE = 256


def nt_dot(a, b):
    return lax.dot_general(a, b, (((1,), (1,)), ((), ())), preferred_element_type=jnp.float32)


def project_and_pack(
    cluster_ref, index_ref, emb_hbm, basis_hbm, send_ref, lane_ref,
    emb, basis, rows, place, emb_sem, basis_sem, *, depth, clusters, total,
):
    n_rows, width = emb.shape
    features = basis.shape[1]
    step = n_rows // CHUNKS

    def emb_copy(k):
        part = pl.ds(k * step, step)
        return pltpu.make_async_copy(emb_hbm.at[part], emb.at[part], emb_sem.at[k])

    basis_copy = pltpu.make_async_copy(basis_hbm, basis, basis_sem)
    basis_copy.start()
    for k in range(CHUNKS):
        emb_copy(k).start()

    cluster = cluster_ref[...]
    blocks = n_rows // LANES
    cluster_iota = lax.broadcasted_iota(jnp.int32, (clusters, n_rows), 0)
    member = cluster_iota == cluster
    member_f = member.astype(jnp.float32)
    stacked = jnp.concatenate(
        [member_f[:, b * LANES:(b + 1) * LANES] for b in range(blocks)], axis=0
    ).astype(jnp.bfloat16)
    row_id = lax.broadcasted_iota(jnp.int32, (LANES, 2 * LANES), 0)
    col_id = lax.broadcasted_iota(jnp.int32, (LANES, 2 * LANES), 1)
    earlier = ((row_id < col_id) | (col_id >= LANES)).astype(jnp.float32).astype(jnp.bfloat16)
    prefix = jnp.dot(stacked, earlier, preferred_element_type=jnp.float32)
    carry = jnp.zeros((clusters, LANES), jnp.float32)
    ranks = []
    for b in range(blocks):
        part = prefix[b * clusters:(b + 1) * clusters]
        mine = member_f[:, b * LANES:(b + 1) * LANES]
        ranks.append(jnp.sum(mine * (part[:, :LANES] + carry), axis=0, keepdims=True))
        carry = carry + part[:, LANES:]
    rank = jnp.concatenate(ranks, axis=1).astype(jnp.int32)
    me = lax.axis_index("docs") * lax.axis_size("rep") + lax.axis_index("rep")
    lane_ref[...] = rank + (me % (LANES // depth)) * depth

    rank_hot = (
        lax.broadcasted_iota(jnp.int32, (LANES, n_rows), 0) % depth == rank
    ).astype(jnp.float32).astype(jnp.bfloat16)
    order = total - index_ref[...]
    digit_id = lax.broadcasted_iota(jnp.int32, (EXTRA, n_rows), 0)
    digits = jnp.zeros((EXTRA, n_rows), jnp.float32)
    left, digit = total, 0
    while left > 0:
        value = ((order >> (8 * digit)) & (BASE - 1)).astype(jnp.float32)
        digits = jnp.where(digit_id == digit, value, digits)
        left, digit = left // BASE, digit + 1
    masked = jnp.concatenate(
        [jnp.where(cluster == c, digits, 0.0) for c in range(clusters)], axis=0
    ).astype(jnp.bfloat16)
    coded = nt_dot(masked, rank_hot).astype(jnp.bfloat16)
    send_ref[:, 2 * depth:, :] = coded.reshape(clusters, EXTRA, LANES)

    slot = cluster * depth + rank
    tall = 256
    for t in range(clusters * depth // tall):
        ids = lax.broadcasted_iota(jnp.int32, (tall, n_rows), 0) + t * tall
        place[t * tall:(t + 1) * tall, :] = (ids == slot).astype(jnp.float32).astype(jnp.bfloat16)

    basis_copy.wait()
    for k in range(CHUNKS):
        emb_copy(k).wait()
        part = slice(k * step, (k + 1) * step)
        projected = jnp.dot(emb[part, :], basis[...], preferred_element_type=jnp.float32)
        scale = lax.rsqrt(jnp.sum(projected * projected, axis=1, keepdims=True) + 1e-06)
        rows[part, :] = (projected * scale).astype(jnp.bfloat16)
    packed = jnp.dot(place[...], rows[...], preferred_element_type=jnp.float32).astype(jnp.bfloat16)
    send_ref[:, :depth, :] = packed[:, :LANES].reshape(clusters, depth, LANES)
    send_ref[:, depth:2 * depth, :] = packed[:, LANES:].reshape(clusters, depth, LANES)


def nearest_kernel(recv_ref, out_ref, x, col, *, depth):
    n = recv_ref.shape[0]
    slots = n * depth
    group = LANES // depth
    x[:, :LANES] = recv_ref[:, :depth, :].reshape(slots, LANES)
    x[:, LANES:] = recv_ref[:, depth:2 * depth, :].reshape(slots, LANES)
    digit_id = lax.broadcasted_iota(jnp.int32, (n, EXTRA, LANES), 1)
    weight = jnp.where(
        digit_id == 0, 1.0, jnp.where(digit_id == 1, float(BASE), float(BASE * BASE))
    )
    digits = recv_ref[:, 2 * depth:, :].astype(jnp.float32)
    order = jnp.sum(digits * weight, axis=1)
    lane_group = lax.broadcasted_iota(jnp.int32, (1, LANES), 1) // depth
    rows_of = []
    for k in range(slots // LANES):
        row = order[k * group:k * group + 1, :]
        for q in range(1, group):
            row = jnp.where(lane_group == q, order[k * group + q:k * group + q + 1, :], row)
        rows_of.append(row)
    turned = order.T
    for c in range(n):
        col[c * depth:(c + 1) * depth, :] = jnp.broadcast_to(
            turned[:depth, c:c + 1], (depth, LANES)
        )
    tile = 256
    for i in range(slots // tile):
        right = x[i * tile:(i + 1) * tile, :]
        row = [rows_of[2 * i], rows_of[2 * i + 1]]
        best = [jnp.full((8, LANES), -1.0, jnp.float32) for _ in range(2)]
        for j in range(slots // tile):
            scores = nt_dot(x[j * tile:(j + 1) * tile, :], right)
            here = col[j * tile:(j + 1) * tile, :]
            for h in range(2):
                kept = jnp.where(here > row[h], scores[:, h * LANES:(h + 1) * LANES], -1.0)
                best[h] = jnp.maximum(best[h], jnp.max(kept.reshape(tile // 8, 8, LANES), axis=0))
        for h in range(2):
            top = jnp.max(best[h], axis=0, keepdims=True)
            k = 2 * i + h
            for q in range(group):
                out_ref[k * group + q] = top


def collect_kernel(back_ref, cluster_ref, lane_ref, out_ref):
    n = back_ref.shape[0]
    n_rows = cluster_ref.shape[1]
    back = back_ref[...].reshape(n, LANES)
    high = back.astype(jnp.bfloat16)
    rest = back - high.astype(jnp.float32)
    middle = rest.astype(jnp.bfloat16)
    low = (rest - middle.astype(jnp.float32)).astype(jnp.bfloat16)
    hot = (
        lax.broadcasted_iota(jnp.int32, (LANES, n_rows), 0) == lane_ref[...]
    ).astype(jnp.float32).astype(jnp.bfloat16)
    picked = jnp.dot(high, hot, preferred_element_type=jnp.float32)
    picked = picked + jnp.dot(middle, hot, preferred_element_type=jnp.float32)
    picked = picked + jnp.dot(low, hot, preferred_element_type=jnp.float32)
    mine = lax.broadcasted_iota(jnp.int32, (n, n_rows), 0) == cluster_ref[...]
    out_ref[...] = jnp.sum(jnp.where(mine, picked, 0.0), axis=0, keepdims=True)


def on_device(embeddings, pca_basis, cluster, doc_index):
    n_docs = lax.axis_size("docs")
    n_rep = lax.axis_size("rep")
    n_dev = n_docs * n_rep
    doc_rows, width = embeddings.shape
    features = pca_basis.shape[1]
    clusters = CL_DEV * n_docs
    assert clusters == n_dev and features == 2 * LANES
    depth = max(2, 2 * doc_rows // clusters)
    cluster_row = cluster.reshape(1, doc_rows)
    index_row = doc_index.reshape(1, doc_rows)
    vmem = pl.BlockSpec(memory_space=pltpu.VMEM)
    hbm = pl.BlockSpec(memory_space=pl.ANY)
    message = 2 * depth + EXTRA

    def pack(*refs):
        project_and_pack(*refs, depth=depth, clusters=clusters, total=doc_rows * n_dev)

    send, lane = pl.pallas_call(
        pack,
        name="project_and_pack",
        in_specs=[vmem, vmem, hbm, hbm],
        out_specs=[vmem, vmem],
        out_shape=[
            jax.ShapeDtypeStruct((n_dev, message, LANES), jnp.bfloat16),
            jax.ShapeDtypeStruct((1, doc_rows), jnp.int32),
        ],
        scratch_shapes=[
            pltpu.VMEM((doc_rows, width), jnp.bfloat16),
            pltpu.VMEM((width, features), jnp.bfloat16),
            pltpu.VMEM((doc_rows, features), jnp.bfloat16),
            pltpu.VMEM((clusters * depth, doc_rows), jnp.bfloat16),
            pltpu.SemaphoreType.DMA((CHUNKS,)),
            pltpu.SemaphoreType.DMA,
        ],
    )(cluster_row, index_row, embeddings, pca_basis)
    recv = lax.all_to_all(send, AXES, split_axis=0, concat_axis=0, tiled=True)

    def search(*refs):
        nearest_kernel(*refs, depth=depth)

    found = pl.pallas_call(
        search,
        name="nearest",
        in_specs=[vmem],
        out_specs=vmem,
        out_shape=jax.ShapeDtypeStruct((n_dev, 1, LANES), jnp.float32),
        scratch_shapes=[
            pltpu.VMEM((n_dev * depth, features), jnp.bfloat16),
            pltpu.VMEM((n_dev * depth, LANES), jnp.float32),
        ],
    )(recv)
    back = lax.all_to_all(found, AXES, split_axis=0, concat_axis=0, tiled=True)
    nearest = pl.pallas_call(
        collect_kernel,
        name="collect",
        in_specs=[vmem, vmem, vmem],
        out_specs=vmem,
        out_shape=jax.ShapeDtypeStruct((1, doc_rows), jnp.float32),
    )(back, cluster_row, lane)
    return nearest.reshape(doc_rows)


def solution(mesh):
    return jax.shard_map(
        on_device,
        mesh=mesh,
        in_specs=(P(AXES, None), P(), P(AXES, None), P(AXES)),
        out_specs=P(AXES),
        check_vma=False,
    )
```

time: 117 us -> 65.5 us (0.56)
  waiting for transfers between devices: 43.5 us -> 0 us
  blocking collectives: 9.68 us -> 47.1 us
  local copies, waits for them, and re-layouts: 26.2 us -> 0 us
  starting transfers between devices: 23.3 us -> 0 us
  Pallas kernels: 0 us -> 18.1 us
  matrix products: 9.78 us -> 0 us
  other arithmetic: 3.5 us -> 0 us
    all_to_all x5 -> x0, waiting for transfers between devices: 43.5 us -> none  [the longest x1 23.5 us: on_device(): lax.all_to_all(send_rows.reshape(n_docs, n_rep, per_rep * slot_depth, fea...]
    all_to_all x1 -> x2, blocking collectives: 9.68 us -> 47.1 us  [the longest x1 36.8 us: on_device(): recv = lax.all_to_all(send, AXES, split_axis=0, concat_axis=0, tiled=True)]
    all_to_all x5 -> x0, starting transfers between devices: 23.3 us -> none  [the longest x1 7.28 us: on_device(): lax.all_to_all(send_index.reshape(n_docs, n_rep, per_rep * slot_depth), '...]
    pallas_call x0 -> x3, Pallas kernels: none -> 18.1 us  [the longest x1 12.1 us: on_device(): pl.pallas_call(pack, name='project_and_pack', in_specs=[vmem, vmem, hbm,...]
    gather x1 -> x0, local copies, waits for them, and re-layouts: 10.5 us -> none  [on_device(): nearest = returned.reshape(-1)[slot_of]]
    scatter x2 -> x0, local copies, waits for them, and re-layouts: 10.5 us -> none  [the longest x1 6.03 us: on_device(): jnp.zeros((clusters * slot_depth, features), jnp.bfloat16).at[slot_of]]
    dot_general x3 -> x0, matrix products: 9.78 us -> none  [the longest x1 5.76 us: on_device(): jnp.dot(embeddings, pca_basis, preferred_element_type=jnp.float32)]
    all_to_all x4 -> x0, other arithmetic: 2.68 us -> none  [the longest x1 0.68 us: on_device(): lax.all_to_all(lax.all_to_all(send_index.reshape(n_docs, n_rep, per_rep *...]
  transfers between devices with their start and end apart: 5 -> 0, of which waited for: 4 -> 0; matrix products, arithmetic and copies ran while one was open for 14% -> 0% of each run, Pallas kernels for 0% -> 0%
where the time goes in v1:
time: 65.5 us; the launch traced here: 65.2 us
  blocking collectives  47.1 us (72%)
  Pallas kernels  18.1 us (28%)
    all_to_all x1, blocking collectives, on_device(): recv = lax.all_to_all(send, AXES, split_axis=0, concat_axis=0, tiled=True)  36.8 us
    pallas_call x1, Pallas kernels, on_device(): pl.pallas_call(pack, name='project_and_pack', in_specs=[vmem, vmem, hbm,...  12.1 us
    all_to_all x1, blocking collectives, on_device(): back = lax.all_to_all(found, AXES, split_axis=0, concat_axis=0, tiled=True)  10.3 us
    pallas_call x1, Pallas kernels, on_device(): pl.pallas_call(search, name='nearest', in_specs=[vmem], out_specs=vmem, o...  4.32 us
    pallas_call x1, Pallas kernels, on_device(): pl.pallas_call(collect_kernel, name='collect', in_specs=[vmem, vmem, vmem...  1.67 us

profile of v1, /device:TPU:0, one launch (start us, length us, event | category | flops | bytes accessed | tf_op | source)
XLA Modules:
  0.0 65.2 jit_solution(1251342585999364941)
XLA Ops:
  0.0 12.1 %project_and_pack.1 = (bf16[32,136,128]{2,1,0:T(8,128)(2,1)}, s32[1,1024]{1,0:T(1,128)}) custom-call(s32[1,1024]{1,0:T(1,128)} %bitcast.3, s32[1,1024]{1,0:T(1,128)} %bitcast.5, bf16[1024,4096]{1,0:T(8,128)(2,1)} %refs_2_.1, bf16[4096,256]{1,0:T(8,128)(2,1)} %refs_3_.1), custom_call_target="tpu_custom_call" | custom-call | tf_op jit(solution)/shard_map/project_and_pack/pallas_call | solution.py:173
  12.1 36.8 %all_to_all.10.refs_0_ = bf16[32,136,128]{2,1,0:T(8,128)(2,1)} all-to-all(bf16[32,136,128]{2,1,0:T(8,128)(2,1)} %get-tuple-element.7), channel_id=1, replica_groups=mesh['docs'=8,'rep'=4] {'docs','rep'}, dimensions={0} | all-to-all | bytes 2228224 | tf_op jit(solution)/shard_map/all_to_all | solution.py:191
  48.9 4.3 %nearest.1 = f32[32,1,128]{2,1,0:T(1,128)} custom-call(bf16[32,136,128]{2,1,0:T(8,128)(2,1)} %all_to_all.10.refs_0_), custom_call_target="tpu_custom_call" | custom-call | tf_op jit(solution)/shard_map/nearest/pallas_call | solution.py:196
  53.2 10.3 %all_to_all.11.back_ref = f32[32,1,128]{2,1,0:T(1,128)} all-to-all(f32[32,1,128]{2,1,0:T(1,128)} %nearest.1), channel_id=1, replica_groups=mesh['docs'=8,'rep'=4] {'docs','rep'}, dimensions={0} | all-to-all | bytes 32768 | tf_op jit(solution)/shard_map/all_to_all | solution.py:207
  63.5 1.7 %collect.1 = f32[1,1024]{1,0:T(1,128)} custom-call(f32[32,1,128]{2,1,0:T(1,128)} %all_to_all.11.back_ref, s32[1,1024]{1,0:T(1,128)} %bitcast.4, s32[1,1024]{1,0:T(1,128)} %get-tuple-element.8.lane_ref), custom_call_target="tpu_custom_call" | custom-call | tf_op jit(solution)/shard_map/collect/pallas_call | solution.py:208

commit v2 on v1

--- a/solution.py
+++ b/solution.py
@@ -18,8 +18,8 @@
 
 
 def project_and_pack(
-    cluster_ref, index_ref, emb_hbm, basis_hbm, send_ref, lane_ref,
-    emb, basis, rows, place, emb_sem, basis_sem, *, depth, clusters, total,
+    cluster_hbm, index_hbm, emb_hbm, basis_hbm, send_ref, lane_ref,
+    cluster_ref, index_ref, emb, basis, rows, place, emb_sem, basis_sem, id_sem, *, depth, clusters, total,
 ):
     n_rows, width = emb.shape
     features = basis.shape[1]
@@ -29,11 +29,17 @@
         part = pl.ds(k * step, step)
         return pltpu.make_async_copy(emb_hbm.at[part], emb.at[part], emb_sem.at[k])
 
+    cluster_copy = pltpu.make_async_copy(cluster_hbm, cluster_ref, id_sem.at[0])
+    index_copy = pltpu.make_async_copy(index_hbm, index_ref, id_sem.at[1])
+    cluster_copy.start()
+    index_copy.start()
     basis_copy = pltpu.make_async_copy(basis_hbm, basis, basis_sem)
     basis_copy.start()
     for k in range(CHUNKS):
         emb_copy(k).start()
 
+    cluster_copy.wait()
+    index_copy.wait()
     cluster = cluster_ref[...]
     blocks = n_rows // LANES
     cluster_iota = lax.broadcasted_iota(jnp.int32, (clusters, n_rows), 0)
@@ -74,15 +80,19 @@
     coded = nt_dot(masked, rank_hot).astype(jnp.bfloat16)
     send_ref[:, 2 * depth:, :] = coded.reshape(clusters, EXTRA, LANES)
 
-    slot = cluster * depth + rank
-    tall = 256
-    for t in range(clusters * depth // tall):
-        ids = lax.broadcasted_iota(jnp.int32, (tall, n_rows), 0) + t * tall
-        place[t * tall:(t + 1) * tall, :] = (ids == slot).astype(jnp.float32).astype(jnp.bfloat16)
+    seat = lax.broadcasted_iota(jnp.int32, (depth, n_rows), 0).astype(jnp.float32).astype(jnp.bfloat16)
+    one = jnp.ones((depth, n_rows), jnp.bfloat16)
+    none = jnp.zeros((depth, n_rows), jnp.bfloat16)
+    for c in range(clusters):
+        here = jnp.where(cluster == c, rank.astype(jnp.float32), -1.0).astype(jnp.bfloat16)
+        place[c * depth:(c + 1) * depth, :] = jnp.where(seat == here, one, none)
 
     basis_copy.wait()
     for k in range(CHUNKS):
         emb_copy(k).wait()
+    halves = 2
+    step = n_rows // halves
+    for k in range(halves):
         part = slice(k * step, (k + 1) * step)
         projected = jnp.dot(emb[part, :], basis[...], preferred_element_type=jnp.float32)
         scale = lax.rsqrt(jnp.sum(projected * projected, axis=1, keepdims=True) + 1e-06)
@@ -164,7 +174,7 @@
     cluster_row = cluster.reshape(1, doc_rows)
     index_row = doc_index.reshape(1, doc_rows)
     vmem = pl.BlockSpec(memory_space=pltpu.VMEM)
-    hbm = pl.BlockSpec(memory_space=pl.ANY)
+    hbm = pl.BlockSpec(memory_space=pltpu.HBM)
     message = 2 * depth + EXTRA
 
     def pack(*refs):
@@ -173,21 +183,25 @@
     send, lane = pl.pallas_call(
         pack,
         name="project_and_pack",
-        in_specs=[vmem, vmem, hbm, hbm],
+        compiler_params=pltpu.CompilerParams(vmem_limit_bytes=28 * 2**20),
+        in_specs=[hbm, hbm, hbm, hbm],
         out_specs=[vmem, vmem],
         out_shape=[
             jax.ShapeDtypeStruct((n_dev, message, LANES), jnp.bfloat16),
             jax.ShapeDtypeStruct((1, doc_rows), jnp.int32),
         ],
         scratch_shapes=[
+            pltpu.VMEM((1, doc_rows), jnp.int32),
+            pltpu.VMEM((1, doc_rows), jnp.int32),
             pltpu.VMEM((doc_rows, width), jnp.bfloat16),
             pltpu.VMEM((width, features), jnp.bfloat16),
             pltpu.VMEM((doc_rows, features), jnp.bfloat16),
             pltpu.VMEM((clusters * depth, doc_rows), jnp.bfloat16),
             pltpu.SemaphoreType.DMA((CHUNKS,)),
             pltpu.SemaphoreType.DMA,
+            pltpu.SemaphoreType.DMA((2,)),
         ],
-    )(cluster_row, index_row, embeddings, pca_basis)
+    )(*[pltpu.with_memory_space_constraint(a, pltpu.HBM) for a in (cluster_row, index_row, embeddings, pca_basis)])
     recv = lax.all_to_all(send, AXES, split_axis=0, concat_axis=0, tiled=True)
 
     def search(*refs):
@@ -196,6 +210,7 @@
     found = pl.pallas_call(
         search,
         name="nearest",
+        compiler_params=pltpu.CompilerParams(vmem_limit_bytes=16 * 2**20),
         in_specs=[vmem],
         out_specs=vmem,
         out_shape=jax.ShapeDtypeStruct((n_dev, 1, LANES), jnp.float32),
@@ -208,6 +223,7 @@
     nearest = pl.pallas_call(
         collect_kernel,
         name="collect",
+        compiler_params=pltpu.CompilerParams(vmem_limit_bytes=8 * 2**20),
         in_specs=[vmem, vmem, vmem],
         out_specs=vmem,
         out_shape=jax.ShapeDtypeStruct((1, doc_rows), jnp.float32),

time: 65.5 us -> 56.8 us (0.87)
  Pallas kernels: 18.1 us -> 11.3 us
  blocking collectives: 47.1 us -> 45.4 us
    pallas_call x3, Pallas kernels: 18.1 us -> 11.3 us  [the longest x1 7.85 us: on_device(): pl.pallas_call(pack, name='project_and_pack', compiler_params=pltpu.Compi...]
    all_to_all x1, blocking collectives: 10.3 us -> 8.89 us  [on_device(): back = lax.all_to_all(found, AXES, split_axis=0, concat_axis=0, tiled=True)]
where the time goes in v2:
time: 56.8 us; the launch traced here: 56.6 us
  blocking collectives  45.4 us (80%)
  Pallas kernels  11.3 us (20%)
    all_to_all x1, blocking collectives, on_device(): recv = lax.all_to_all(send, AXES, split_axis=0, concat_axis=0, tiled=True)  36.5 us
    all_to_all x1, blocking collectives, on_device(): back = lax.all_to_all(found, AXES, split_axis=0, concat_axis=0, tiled=True)  8.89 us
    pallas_call x1, Pallas kernels, on_device(): pl.pallas_call(pack, name='project_and_pack', compiler_params=pltpu.Compi...  7.85 us
    pallas_call x1, Pallas kernels, on_device(): pl.pallas_call(search, name='nearest', compiler_params=pltpu.CompilerPara...  2.46 us

profile of v2, /device:TPU:0, one launch (start us, length us, event | category | flops | bytes accessed | tf_op | source)
XLA Modules:
  0.0 56.6 jit_solution(17715625493571402424)
XLA Ops:
  0.0 7.8 %project_and_pack.1 = (bf16[32,136,128]{2,1,0:T(8,128)(2,1)S(1)}, s32[1,1024]{1,0:T(1,128)S(1)}) custom-call(s32[1,1024]{1,0:T(1,128)} %bitcast.3, s32[1,1024]{1,0:T(1,128)} %bitcast.5, bf16[1024,4096]{1,0:T(8,128)(2,1)} %refs_2_.1, bf16[4096,256]{1,0:T(8,128)(2,1)} %refs_3_.1), custom_call_target="tpu_custom_call" | custom-call | tf_op jit(solution)/shard_map/project_and_pack/pallas_call | solution.py:183
  7.9 0.0 copy-start
  7.9 36.5 %all_to_all.10.refs_0_ = bf16[32,136,128]{2,1,0:T(8,128)(2,1)S(1)} all-to-all(bf16[32,136,128]{2,1,0:T(8,128)(2,1)S(1)} %get-tuple-element.7), channel_id=1, replica_groups=mesh['docs'=8,'rep'=4] {'docs','rep'}, dimensions={0} | all-to-all | bytes 2228224 | tf_op jit(solution)/shard_map/all_to_all | solution.py:205
  44.3 2.5 %nearest.1 = f32[32,1,128]{2,1,0:T(1,128)S(1)} custom-call(bf16[32,136,128]{2,1,0:T(8,128)(2,1)S(1)} %all_to_all.10.refs_0_), custom_call_target="tpu_custom_call" | custom-call | tf_op jit(solution)/shard_map/nearest/pallas_call | solution.py:210
  46.8 8.9 %all_to_all.11.back_ref = f32[32,1,128]{2,1,0:T(1,128)S(1)} all-to-all(f32[32,1,128]{2,1,0:T(1,128)S(1)} %nearest.1), channel_id=1, replica_groups=mesh['docs'=8,'rep'=4] {'docs','rep'}, dimensions={0} | all-to-all | bytes 32768 | tf_op jit(solution)/shard_map/all_to_all | solution.py:222
  55.7 0.0 copy-done
  55.7 0.9 %collect.1 = f32[1,1024]{1,0:T(1,128)} custom-call(f32[32,1,128]{2,1,0:T(1,128)S(1)} %all_to_all.11.back_ref, s32[1,1024]{1,0:T(1,128)S(1)} %bitcast.4, s32[1,1024]{1,0:T(1,128)S(1)} %get-tuple-element.8.lane_ref), custom_call_target="tpu_custom_call" | custom-call | tf_op jit(solution)/shard_map/collect/pallas_call | solution.py:223
Async XLA Ops:
  7.9 47.8 %copy-start = (s32[1024,1]{0,1:T(1,128)S(1)}, s32[1024,1]{0,1:T(1,128)}, u32[]{:S(2)}) copy-start(s32[1024,1]{0,1:T(1,128)} %param.6) | copy-start | bytes 12292

commit v3 on v2

--- a/solution.py
+++ b/solution.py
@@ -10,6 +10,7 @@
 LANES = 128
 EXTRA = 8
 CHUNKS = 8
+FIRST = 4
 BASE = 256
 
 
@@ -36,7 +37,7 @@
     basis_copy = pltpu.make_async_copy(basis_hbm, basis, basis_sem)
     basis_copy.start()
     for k in range(CHUNKS):
-        emb_copy(k).start()
+        emb_copy(k).start(priority=0 if k < FIRST else 1)
 
     cluster_copy.wait()
     index_copy.wait()
@@ -88,12 +89,15 @@
         place[c * depth:(c + 1) * depth, :] = jnp.where(seat == here, one, none)
 
     basis_copy.wait()
-    for k in range(CHUNKS):
-        emb_copy(k).wait()
-    halves = 2
-    step = n_rows // halves
-    for k in range(halves):
-        part = slice(k * step, (k + 1) * step)
+    size = 256
+    for k in range(n_rows // size):
+        if k * size == 0:
+            for q in range(FIRST):
+                emb_copy(q).wait()
+        if k * size == FIRST * step:
+            for q in range(FIRST, CHUNKS):
+                emb_copy(q).wait()
+        part = slice(k * size, (k + 1) * size)
         projected = jnp.dot(emb[part, :], basis[...], preferred_element_type=jnp.float32)
         scale = lax.rsqrt(jnp.sum(projected * projected, axis=1, keepdims=True) + 1e-06)
         rows[part, :] = (projected * scale).astype(jnp.bfloat16)

time: 56.8 us -> 56 us (0.986)
  Pallas kernels: 11.3 us -> 10.4 us
    pallas_call x1, Pallas kernels: 7.85 us -> 7.03 us  [on_device(): pl.pallas_call(pack, name='project_and_pack', compiler_params=pltpu.Compi...]
where the time goes in v3:
time: 56 us; the launch traced here: 55.8 us
  blocking collectives  45.4 us (81%)
  Pallas kernels  10.4 us (19%)
    all_to_all x1, blocking collectives, on_device(): recv = lax.all_to_all(send, AXES, split_axis=0, concat_axis=0, tiled=True)  36.5 us
    all_to_all x1, blocking collectives, on_device(): back = lax.all_to_all(found, AXES, split_axis=0, concat_axis=0, tiled=True)  8.89 us
    pallas_call x1, Pallas kernels, on_device(): pl.pallas_call(pack, name='project_and_pack', compiler_params=pltpu.Compi...  7.03 us
    pallas_call x1, Pallas kernels, on_device(): pl.pallas_call(search, name='nearest', compiler_params=pltpu.CompilerPara...  2.46 us

profile of v3, /device:TPU:0, one launch (start us, length us, event | category | flops | bytes accessed | tf_op | source)
XLA Modules:
  0.0 55.8 jit_solution(2265802680058767)
XLA Ops:
  0.0 7.0 %project_and_pack.1 = (bf16[32,136,128]{2,1,0:T(8,128)(2,1)S(1)}, s32[1,1024]{1,0:T(1,128)S(1)}) custom-call(s32[1,1024]{1,0:T(1,128)} %bitcast.3, s32[1,1024]{1,0:T(1,128)} %bitcast.5, bf16[1024,4096]{1,0:T(8,128)(2,1)} %refs_2_.1, bf16[4096,256]{1,0:T(8,128)(2,1)} %refs_3_.1), custom_call_target="tpu_custom_call" | custom-call | tf_op jit(solution)/shard_map/project_and_pack/pallas_call | solution.py:187
  7.0 0.0 copy-start
  7.1 36.5 %all_to_all.10.refs_0_ = bf16[32,136,128]{2,1,0:T(8,128)(2,1)S(1)} all-to-all(bf16[32,136,128]{2,1,0:T(8,128)(2,1)S(1)} %get-tuple-element.7), channel_id=1, replica_groups=mesh['docs'=8,'rep'=4] {'docs','rep'}, dimensions={0} | all-to-all | bytes 2228224 | tf_op jit(solution)/shard_map/all_to_all | solution.py:209
  43.5 2.5 %nearest.1 = f32[32,1,128]{2,1,0:T(1,128)S(1)} custom-call(bf16[32,136,128]{2,1,0:T(8,128)(2,1)S(1)} %all_to_all.10.refs_0_), custom_call_target="tpu_custom_call" | custom-call | tf_op jit(solution)/shard_map/nearest/pallas_call | solution.py:214
  46.0 8.9 %all_to_all.11.back_ref = f32[32,1,128]{2,1,0:T(1,128)S(1)} all-to-all(f32[32,1,128]{2,1,0:T(1,128)S(1)} %nearest.1), channel_id=1, replica_groups=mesh['docs'=8,'rep'=4] {'docs','rep'}, dimensions={0} | all-to-all | bytes 32768 | tf_op jit(solution)/shard_map/all_to_all | solution.py:226
  54.9 0.0 copy-done
  54.9 0.9 %collect.1 = f32[1,1024]{1,0:T(1,128)} custom-call(f32[32,1,128]{2,1,0:T(1,128)S(1)} %all_to_all.11.back_ref, s32[1,1024]{1,0:T(1,128)S(1)} %bitcast.4, s32[1,1024]{1,0:T(1,128)S(1)} %get-tuple-element.8.lane_ref), custom_call_target="tpu_custom_call" | custom-call | tf_op jit(solution)/shard_map/collect/pallas_call | solution.py:227
Async XLA Ops:
  7.0 47.8 %copy-start = (s32[1024,1]{0,1:T(1,128)S(1)}, s32[1024,1]{0,1:T(1,128)}, u32[]{:S(2)}) copy-start(s32[1024,1]{0,1:T(1,128)} %param.6) | copy-start | bytes 12292

commit v4 on v3

--- a/solution.py
+++ b/solution.py
@@ -8,20 +8,29 @@
 CL_DEV = 4
 AXES = ("docs", "rep")
 LANES = 128
-EXTRA = 8
+PAIR = 2
 CHUNKS = 8
 FIRST = 4
 BASE = 256
 
 
+def extra_rows(total):
+    digits = 1
+    while BASE ** digits <= total:
+        digits += 1
+    return -(-digits // PAIR) * PAIR
+
+
 def nt_dot(a, b):
     return lax.dot_general(a, b, (((1,), (1,)), ((), ())), preferred_element_type=jnp.float32)
 
 
 def project_and_pack(
-    cluster_hbm, index_hbm, emb_hbm, basis_hbm, send_ref, lane_ref,
+    cluster_hbm, index_hbm, emb_hbm, basis_hbm, send_pairs, lane_ref,
     cluster_ref, index_ref, emb, basis, rows, place, emb_sem, basis_sem, id_sem, *, depth, clusters, total,
 ):
+    extra = extra_rows(total)
+    send_ref = send_pairs.reshape(clusters, 2 * depth + extra, LANES)
     n_rows, width = emb.shape
     features = basis.shape[1]
     step = n_rows // CHUNKS
@@ -68,8 +77,8 @@
         lax.broadcasted_iota(jnp.int32, (LANES, n_rows), 0) % depth == rank
     ).astype(jnp.float32).astype(jnp.bfloat16)
     order = total - index_ref[...]
-    digit_id = lax.broadcasted_iota(jnp.int32, (EXTRA, n_rows), 0)
-    digits = jnp.zeros((EXTRA, n_rows), jnp.float32)
+    digit_id = lax.broadcasted_iota(jnp.int32, (extra, n_rows), 0)
+    digits = jnp.zeros((extra, n_rows), jnp.float32)
     left, digit = total, 0
     while left > 0:
         value = ((order >> (8 * digit)) & (BASE - 1)).astype(jnp.float32)
@@ -79,7 +88,8 @@
         [jnp.where(cluster == c, digits, 0.0) for c in range(clusters)], axis=0
     ).astype(jnp.bfloat16)
     coded = nt_dot(masked, rank_hot).astype(jnp.bfloat16)
-    send_ref[:, 2 * depth:, :] = coded.reshape(clusters, EXTRA, LANES)
+    for c in range(clusters):
+        send_ref[c, 2 * depth:, :] = coded[c * extra:(c + 1) * extra, :]
 
     seat = lax.broadcasted_iota(jnp.int32, (depth, n_rows), 0).astype(jnp.float32).astype(jnp.bfloat16)
     one = jnp.ones((depth, n_rows), jnp.bfloat16)
@@ -106,13 +116,15 @@
     send_ref[:, depth:2 * depth, :] = packed[:, LANES:].reshape(clusters, depth, LANES)
 
 
-def nearest_kernel(recv_ref, out_ref, x, col, *, depth):
-    n = recv_ref.shape[0]
+def nearest_kernel(recv_pairs, out_ref, x, col, *, depth):
+    n, pairs = recv_pairs.shape[:2]
+    recv_ref = recv_pairs.reshape(n, pairs * PAIR, LANES)
+    extra = pairs * PAIR - 2 * depth
     slots = n * depth
     group = LANES // depth
     x[:, :LANES] = recv_ref[:, :depth, :].reshape(slots, LANES)
     x[:, LANES:] = recv_ref[:, depth:2 * depth, :].reshape(slots, LANES)
-    digit_id = lax.broadcasted_iota(jnp.int32, (n, EXTRA, LANES), 1)
+    digit_id = lax.broadcasted_iota(jnp.int32, (n, extra, LANES), 1)
     weight = jnp.where(
         digit_id == 0, 1.0, jnp.where(digit_id == 1, float(BASE), float(BASE * BASE))
     )
@@ -179,7 +191,7 @@
     index_row = doc_index.reshape(1, doc_rows)
     vmem = pl.BlockSpec(memory_space=pltpu.VMEM)
     hbm = pl.BlockSpec(memory_space=pltpu.HBM)
-    message = 2 * depth + EXTRA
+    message = 2 * depth + extra_rows(doc_rows * n_dev)
 
     def pack(*refs):
         project_and_pack(*refs, depth=depth, clusters=clusters, total=doc_rows * n_dev)
@@ -191,7 +203,7 @@
         in_specs=[hbm, hbm, hbm, hbm],
         out_specs=[vmem, vmem],
         out_shape=[
-            jax.ShapeDtypeStruct((n_dev, message, LANES), jnp.bfloat16),
+            jax.ShapeDtypeStruct((n_dev, message // PAIR, PAIR, LANES), jnp.bfloat16),
             jax.ShapeDtypeStruct((1, doc_rows), jnp.int32),
         ],
         scratch_shapes=[

time: 56 us -> 55.6 us (level)
  blocking collectives: 45.4 us -> 44.4 us
  Pallas kernels: 10.4 us -> 11 us
    all_to_all x1, blocking collectives: 36.5 us -> 35.5 us  [on_device(): recv = lax.all_to_all(send, AXES, split_axis=0, concat_axis=0, tiled=True)]
where the time goes in v4:
time: 55.6 us; the launch traced here: 55.4 us
  blocking collectives  44.4 us (80%)
  Pallas kernels  11 us (20%)
    all_to_all x1, blocking collectives, on_device(): recv = lax.all_to_all(send, AXES, split_axis=0, concat_axis=0, tiled=True)  35.5 us
    all_to_all x1, blocking collectives, on_device(): back = lax.all_to_all(found, AXES, split_axis=0, concat_axis=0, tiled=True)  8.87 us
    pallas_call x1, Pallas kernels, on_device(): pl.pallas_call(pack, name='project_and_pack', compiler_params=pltpu.Compi...  7.24 us
    pallas_call x1, Pallas kernels, on_device(): pl.pallas_call(search, name='nearest', compiler_params=pltpu.CompilerPara...  2.86 us

profile of v4, /device:TPU:0, one launch (start us, length us, event | category | flops | bytes accessed | tf_op | source)
XLA Modules:
  0.0 55.4 jit_solution(8294329945961780855)
XLA Ops:
  0.0 7.2 %project_and_pack.1 = (bf16[32,65,2,128]{3,2,1,0:T(2,128)(2,1)S(1)}, s32[1,1024]{1,0:T(1,128)S(1)}) custom-call(s32[1,1024]{1,0:T(1,128)} %bitcast.3, s32[1,1024]{1,0:T(1,128)} %bitcast.5, bf16[1024,4096]{1,0:T(8,128)(2,1)} %refs_2_.1, bf16[4096,256]{1,0:T(8,128)(2,1)} %refs_3_.1), custom_call_target="tpu_custom_call" | custom-call | tf_op jit(solution)/shard_map/project_and_pack/pallas_call | solution.py:199
  7.2 0.0 copy-start
  7.3 35.5 %all_to_all.10.refs_0_ = bf16[32,65,2,128]{3,2,1,0:T(2,128)(2,1)S(1)} all-to-all(bf16[32,65,2,128]{3,2,1,0:T(2,128)(2,1)S(1)} %get-tuple-element.7), channel_id=1, replica_groups=mesh['docs'=8,'rep'=4] {'docs','rep'}, dimensions={0} | all-to-all | bytes 2129920 | tf_op jit(solution)/shard_map/all_to_all | solution.py:221
  42.8 2.9 %nearest.1 = f32[32,1,128]{2,1,0:T(1,128)S(1)} custom-call(bf16[32,65,2,128]{3,2,1,0:T(2,128)(2,1)S(1)} %all_to_all.10.refs_0_), custom_call_target="tpu_custom_call" | custom-call | tf_op jit(solution)/shard_map/nearest/pallas_call | solution.py:226
  45.6 8.9 %all_to_all.11.back_ref = f32[32,1,128]{2,1,0:T(1,128)S(1)} all-to-all(f32[32,1,128]{2,1,0:T(1,128)S(1)} %nearest.1), channel_id=1, replica_groups=mesh['docs'=8,'rep'=4] {'docs','rep'}, dimensions={0} | all-to-all | bytes 32768 | tf_op jit(solution)/shard_map/all_to_all | solution.py:238
  54.5 0.0 copy-done
  54.5 0.9 %collect.1 = f32[1,1024]{1,0:T(1,128)} custom-call(f32[32,1,128]{2,1,0:T(1,128)S(1)} %all_to_all.11.back_ref, s32[1,1024]{1,0:T(1,128)S(1)} %bitcast.4, s32[1,1024]{1,0:T(1,128)S(1)} %get-tuple-element.8.lane_ref), custom_call_target="tpu_custom_call" | custom-call | tf_op jit(solution)/shard_map/collect/pallas_call | solution.py:239
Async XLA Ops:
  7.2 47.2 %copy-start = (s32[1024,1]{0,1:T(1,128)S(1)}, s32[1024,1]{0,1:T(1,128)}, u32[]{:S(2)}) copy-start(s32[1024,1]{0,1:T(1,128)} %param.6) | copy-start | bytes 12292

commit v5 on v4

--- a/solution.py
+++ b/solution.py
@@ -8,7 +8,7 @@
 CL_DEV = 4
 AXES = ("docs", "rep")
 LANES = 128
-PAIR = 2
+ROWS = 4
 CHUNKS = 8
 FIRST = 4
 BASE = 256
@@ -18,7 +18,7 @@
     digits = 1
     while BASE ** digits <= total:
         digits += 1
-    return -(-digits // PAIR) * PAIR
+    return -(-digits // ROWS) * ROWS
 
 
 def nt_dot(a, b):
@@ -26,11 +26,11 @@
 
 
 def project_and_pack(
-    cluster_hbm, index_hbm, emb_hbm, basis_hbm, send_pairs, lane_ref,
+    cluster_hbm, index_hbm, emb_hbm, basis_hbm, send_rows, lane_ref,
     cluster_ref, index_ref, emb, basis, rows, place, emb_sem, basis_sem, id_sem, *, depth, clusters, total,
 ):
     extra = extra_rows(total)
-    send_ref = send_pairs.reshape(clusters, 2 * depth + extra, LANES)
+    send_ref = send_rows.reshape(clusters, 2 * depth + extra, LANES)
     n_rows, width = emb.shape
     features = basis.shape[1]
     step = n_rows // CHUNKS
@@ -116,10 +116,10 @@
     send_ref[:, depth:2 * depth, :] = packed[:, LANES:].reshape(clusters, depth, LANES)
 
 
-def nearest_kernel(recv_pairs, out_ref, x, col, *, depth):
-    n, pairs = recv_pairs.shape[:2]
-    recv_ref = recv_pairs.reshape(n, pairs * PAIR, LANES)
-    extra = pairs * PAIR - 2 * depth
+def nearest_kernel(recv_rows, out_ref, x, col, side, *, depth):
+    n, groups = recv_rows.shape[:2]
+    recv_ref = recv_rows.reshape(n, groups * ROWS, LANES)
+    extra = groups * ROWS - 2 * depth
     slots = n * depth
     group = LANES // depth
     x[:, :LANES] = recv_ref[:, :depth, :].reshape(slots, LANES)
@@ -143,21 +143,40 @@
             turned[:depth, c:c + 1], (depth, LANES)
         )
     tile = 256
-    for i in range(slots // tile):
+    tiles = slots // tile
+    tops = {}
+    for i in range(tiles):
         right = x[i * tile:(i + 1) * tile, :]
-        row = [rows_of[2 * i], rows_of[2 * i + 1]]
         best = [jnp.full((8, LANES), -1.0, jnp.float32) for _ in range(2)]
-        for j in range(slots // tile):
+        for j in range(i + 1):
             scores = nt_dot(x[j * tile:(j + 1) * tile, :], right)
-            here = col[j * tile:(j + 1) * tile, :]
+            part = slice(j * tile, (j + 1) * tile)
+            here = col[part, :]
+            mirrored = None
             for h in range(2):
-                kept = jnp.where(here > row[h], scores[:, h * LANES:(h + 1) * LANES], -1.0)
+                mine = scores[:, h * LANES:(h + 1) * LANES]
+                before = here > rows_of[2 * i + h]
+                kept = jnp.where(before, mine, -1.0)
                 best[h] = jnp.maximum(best[h], jnp.max(kept.reshape(tile // 8, 8, LANES), axis=0))
+                if j < i:
+                    other = jnp.where(before, -1.0, mine)
+                    mirrored = other if mirrored is None else jnp.maximum(mirrored, other)
+            if j < i:
+                if i > j + 1:
+                    mirrored = jnp.maximum(mirrored, side[part, :])
+                if i < tiles - 1:
+                    side[part, :] = mirrored
+                else:
+                    for h in range(2):
+                        turned_side = mirrored[h * LANES:(h + 1) * LANES, :].T
+                        tops[2 * j + h] = jnp.maximum(
+                            tops[2 * j + h], jnp.max(turned_side, axis=0, keepdims=True)
+                        )
         for h in range(2):
-            top = jnp.max(best[h], axis=0, keepdims=True)
-            k = 2 * i + h
-            for q in range(group):
-                out_ref[k * group + q] = top
+            tops[2 * i + h] = jnp.max(best[h], axis=0, keepdims=True)
+    for k in range(slots // LANES):
+        for q in range(group):
+            out_ref[k * group + q] = tops[k]
 
 
 def collect_kernel(back_ref, cluster_ref, lane_ref, out_ref):
@@ -203,7 +222,7 @@
         in_specs=[hbm, hbm, hbm, hbm],
         out_specs=[vmem, vmem],
         out_shape=[
-            jax.ShapeDtypeStruct((n_dev, message // PAIR, PAIR, LANES), jnp.bfloat16),
+            jax.ShapeDtypeStruct((n_dev, message // ROWS, ROWS, LANES), jnp.bfloat16),
             jax.ShapeDtypeStruct((1, doc_rows), jnp.int32),
         ],
         scratch_shapes=[
@@ -233,6 +252,7 @@
         scratch_shapes=[
             pltpu.VMEM((n_dev * depth, features), jnp.bfloat16),
             pltpu.VMEM((n_dev * depth, LANES), jnp.float32),
+            pltpu.VMEM((n_dev * depth, LANES), jnp.float32),
         ],
     )(recv)
     back = lax.all_to_all(found, AXES, split_axis=0, concat_axis=0, tiled=True)

time: 55.6 us -> 55 us (0.989)
  Pallas kernels: 11 us -> 10.1 us
    pallas_call x1, Pallas kernels: 2.86 us -> 2.2 us  [on_device(): pl.pallas_call(search, name='nearest', compiler_params=pltpu.CompilerPara...]
where the time goes in v5:
time: 55 us; the launch traced here: 54.8 us
  blocking collectives  44.7 us (81%)
  Pallas kernels  10.1 us (18%)
    all_to_all x1, blocking collectives, on_device(): recv = lax.all_to_all(send, AXES, split_axis=0, concat_axis=0, tiled=True)  35.8 us
    all_to_all x1, blocking collectives, on_device(): back = lax.all_to_all(found, AXES, split_axis=0, concat_axis=0, tiled=True)  8.87 us
    pallas_call x1, Pallas kernels, on_device(): pl.pallas_call(pack, name='project_and_pack', compiler_params=pltpu.Compi...  6.98 us
    pallas_call x1, Pallas kernels, on_device(): pl.pallas_call(search, name='nearest', compiler_params=pltpu.CompilerPara...  2.2 us

profile of v5, /device:TPU:0, one launch (start us, length us, event | category | flops | bytes accessed | tf_op | source)
XLA Modules:
  0.0 54.8 jit_solution(6903850937083661483)
XLA Ops:
  0.0 7.0 %project_and_pack.1 = (bf16[32,33,4,128]{3,2,1,0:T(4,128)(2,1)S(1)}, s32[1,1024]{1,0:T(1,128)S(1)}) custom-call(s32[1,1024]{1,0:T(1,128)} %bitcast.3, s32[1,1024]{1,0:T(1,128)} %bitcast.5, bf16[1024,4096]{1,0:T(8,128)(2,1)} %refs_2_.1, bf16[4096,256]{1,0:T(8,128)(2,1)} %refs_3_.1), custom_call_target="tpu_custom_call" | custom-call | tf_op jit(solution)/shard_map/project_and_pack/pallas_call | solution.py:218
  7.0 0.0 copy-start
  7.0 35.8 %all_to_all.10.refs_0_ = bf16[32,33,4,128]{3,2,1,0:T(4,128)(2,1)S(1)} all-to-all(bf16[32,33,4,128]{3,2,1,0:T(4,128)(2,1)S(1)} %get-tuple-element.7), channel_id=1, replica_groups=mesh['docs'=8,'rep'=4] {'docs','rep'}, dimensions={0} | all-to-all | bytes 2162688 | tf_op jit(solution)/shard_map/all_to_all | solution.py:240
  42.8 2.2 %nearest.1 = f32[32,1,128]{2,1,0:T(1,128)S(1)} custom-call(bf16[32,33,4,128]{3,2,1,0:T(4,128)(2,1)S(1)} %all_to_all.10.refs_0_), custom_call_target="tpu_custom_call" | custom-call | tf_op jit(solution)/shard_map/nearest/pallas_call | solution.py:245
  45.0 8.9 %all_to_all.11.back_ref = f32[32,1,128]{2,1,0:T(1,128)S(1)} all-to-all(f32[32,1,128]{2,1,0:T(1,128)S(1)} %nearest.1), channel_id=1, replica_groups=mesh['docs'=8,'rep'=4] {'docs','rep'}, dimensions={0} | all-to-all | bytes 32768 | tf_op jit(solution)/shard_map/all_to_all | solution.py:258
  53.9 0.0 copy-done
  53.9 0.9 %collect.1 = f32[1,1024]{1,0:T(1,128)} custom-call(f32[32,1,128]{2,1,0:T(1,128)S(1)} %all_to_all.11.back_ref, s32[1,1024]{1,0:T(1,128)S(1)} %bitcast.4, s32[1,1024]{1,0:T(1,128)S(1)} %get-tuple-element.8.lane_ref), custom_call_target="tpu_custom_call" | custom-call | tf_op jit(solution)/shard_map/collect/pallas_call | solution.py:259
Async XLA Ops:
  7.0 46.9 %copy-start = (s32[1024,1]{0,1:T(1,128)S(1)}, s32[1024,1]{0,1:T(1,128)}, u32[]{:S(2)}) copy-start(s32[1024,1]{0,1:T(1,128)} %param.6) | copy-start | bytes 12292

commit v6 on v5

--- a/solution.py
+++ b/solution.py
@@ -111,9 +111,15 @@
         projected = jnp.dot(emb[part, :], basis[...], preferred_element_type=jnp.float32)
         scale = lax.rsqrt(jnp.sum(projected * projected, axis=1, keepdims=True) + 1e-06)
         rows[part, :] = (projected * scale).astype(jnp.bfloat16)
-    packed = jnp.dot(place[...], rows[...], preferred_element_type=jnp.float32).astype(jnp.bfloat16)
-    send_ref[:, :depth, :] = packed[:, :LANES].reshape(clusters, depth, LANES)
-    send_ref[:, depth:2 * depth, :] = packed[:, LANES:].reshape(clusters, depth, LANES)
+    tall = min(512, clusters * depth)
+    per = tall // depth
+    for t in range(clusters // per):
+        packed = jnp.dot(
+            place[t * tall:(t + 1) * tall, :], rows[...], preferred_element_type=jnp.float32
+        ).astype(jnp.bfloat16)
+        some = slice(t * per, (t + 1) * per)
+        send_ref[some, :depth, :] = packed[:, :LANES].reshape(per, depth, LANES)
+        send_ref[some, depth:2 * depth, :] = packed[:, LANES:].reshape(per, depth, LANES)
 
 
 def nearest_kernel(recv_rows, out_ref, x, col, side, *, depth):
@@ -190,9 +196,10 @@
     hot = (
         lax.broadcasted_iota(jnp.int32, (LANES, n_rows), 0) == lane_ref[...]
     ).astype(jnp.float32).astype(jnp.bfloat16)
-    picked = jnp.dot(high, hot, preferred_element_type=jnp.float32)
-    picked = picked + jnp.dot(middle, hot, preferred_element_type=jnp.float32)
-    picked = picked + jnp.dot(low, hot, preferred_element_type=jnp.float32)
+    parts = jnp.dot(
+        jnp.concatenate([high, middle, low], axis=0), hot, preferred_element_type=jnp.float32
+    )
+    picked = parts[:n] + parts[n:2 * n] + parts[2 * n:]
     mine = lax.broadcasted_iota(jnp.int32, (n, n_rows), 0) == cluster_ref[...]
     out_ref[...] = jnp.sum(jnp.where(mine, picked, 0.0), axis=0, keepdims=True)
 

time: 55 us -> 54.8 us (level)
  no operation moved by 1% of the time
where the time goes in v6:
time: 54.8 us; the launch traced here: 54.6 us
  blocking collectives  44.7 us (82%)
  Pallas kernels  9.87 us (18%)
    all_to_all x1, blocking collectives, on_device(): recv = lax.all_to_all(send, AXES, split_axis=0, concat_axis=0, tiled=True)  35.8 us
    all_to_all x1, blocking collectives, on_device(): back = lax.all_to_all(found, AXES, split_axis=0, concat_axis=0, tiled=True)  8.87 us
    pallas_call x1, Pallas kernels, on_device(): pl.pallas_call(pack, name='project_and_pack', compiler_params=pltpu.Compi...  6.81 us
    pallas_call x1, Pallas kernels, on_device(): pl.pallas_call(search, name='nearest', compiler_params=pltpu.CompilerPara...  2.2 us

profile of v6, /device:TPU:0, one launch (start us, length us, event | category | flops | bytes accessed | tf_op | source)
XLA Modules:
  0.0 54.6 jit_solution(449805583288363256)
XLA Ops:
  0.0 6.8 %project_and_pack.1 = (bf16[32,33,4,128]{3,2,1,0:T(4,128)(2,1)S(1)}, s32[1,1024]{1,0:T(1,128)S(1)}) custom-call(s32[1,1024]{1,0:T(1,128)} %bitcast.3, s32[1,1024]{1,0:T(1,128)} %bitcast.5, bf16[1024,4096]{1,0:T(8,128)(2,1)} %refs_2_.1, bf16[4096,256]{1,0:T(8,128)(2,1)} %refs_3_.1), custom_call_target="tpu_custom_call" | custom-call | tf_op jit(solution)/shard_map/project_and_pack/pallas_call | solution.py:225
  6.8 0.0 copy-start
  6.8 35.8 %all_to_all.10.refs_0_ = bf16[32,33,4,128]{3,2,1,0:T(4,128)(2,1)S(1)} all-to-all(bf16[32,33,4,128]{3,2,1,0:T(4,128)(2,1)S(1)} %get-tuple-element.7), channel_id=1, replica_groups=mesh['docs'=8,'rep'=4] {'docs','rep'}, dimensions={0} | all-to-all | bytes 2162688 | tf_op jit(solution)/shard_map/all_to_all | solution.py:247
  42.7 2.2 %nearest.1 = f32[32,1,128]{2,1,0:T(1,128)S(1)} custom-call(bf16[32,33,4,128]{3,2,1,0:T(4,128)(2,1)S(1)} %all_to_all.10.refs_0_), custom_call_target="tpu_custom_call" | custom-call | tf_op jit(solution)/shard_map/nearest/pallas_call | solution.py:252
  44.9 8.9 %all_to_all.11.back_ref = f32[32,1,128]{2,1,0:T(1,128)S(1)} all-to-all(f32[32,1,128]{2,1,0:T(1,128)S(1)} %nearest.1), channel_id=1, replica_groups=mesh['docs'=8,'rep'=4] {'docs','rep'}, dimensions={0} | all-to-all | bytes 32768 | tf_op jit(solution)/shard_map/all_to_all | solution.py:265
  53.7 0.0 copy-done
  53.7 0.9 %collect.1 = f32[1,1024]{1,0:T(1,128)} custom-call(f32[32,1,128]{2,1,0:T(1,128)S(1)} %all_to_all.11.back_ref, s32[1,1024]{1,0:T(1,128)S(1)} %bitcast.4, s32[1,1024]{1,0:T(1,128)S(1)} %get-tuple-element.8.lane_ref), custom_call_target="tpu_custom_call" | custom-call | tf_op jit(solution)/shard_map/collect/pallas_call | solution.py:266
Async XLA Ops:
  6.8 46.9 %copy-start = (s32[1024,1]{0,1:T(1,128)S(1)}, s32[1024,1]{0,1:T(1,128)}, u32[]{:S(2)}) copy-start(s32[1024,1]{0,1:T(1,128)} %param.6) | copy-start | bytes 12292

commit v7 on v6

--- a/solution.py
+++ b/solution.py
@@ -9,8 +9,7 @@
 AXES = ("docs", "rep")
 LANES = 128
 ROWS = 4
-CHUNKS = 8
-FIRST = 4
+CHUNKS = 2
 BASE = 256
 
 
@@ -27,7 +26,7 @@
 
 def project_and_pack(
     cluster_hbm, index_hbm, emb_hbm, basis_hbm, send_rows, lane_ref,
-    cluster_ref, index_ref, emb, basis, rows, place, emb_sem, basis_sem, id_sem, *, depth, clusters, total,
+    cluster_ref, index_ref, emb, basis, partial, rows, place, emb_sem, basis_sem, id_sem, *, depth, clusters, total,
 ):
     extra = extra_rows(total)
     send_ref = send_rows.reshape(clusters, 2 * depth + extra, LANES)
@@ -35,18 +34,28 @@
     features = basis.shape[1]
     step = n_rows // CHUNKS
 
-    def emb_copy(k):
+    split = width * 1 // 2
+    spans = [slice(0, split), slice(split, width)]
+
+    def basis_copy(h):
+        part = pl.ds(spans[h].start, spans[h].stop - spans[h].start)
+        return pltpu.make_async_copy(basis_hbm.at[part], basis.at[part], basis_sem.at[h])
+
+    def emb_copy(h, k):
         part = pl.ds(k * step, step)
-        return pltpu.make_async_copy(emb_hbm.at[part], emb.at[part], emb_sem.at[k])
+        cols = pl.ds(spans[h].start, spans[h].stop - spans[h].start)
+        return pltpu.make_async_copy(
+            emb_hbm.at[part, cols], emb.at[part, cols], emb_sem.at[h, k]
+        )
 
     cluster_copy = pltpu.make_async_copy(cluster_hbm, cluster_ref, id_sem.at[0])
     index_copy = pltpu.make_async_copy(index_hbm, index_ref, id_sem.at[1])
     cluster_copy.start()
     index_copy.start()
-    basis_copy = pltpu.make_async_copy(basis_hbm, basis, basis_sem)
-    basis_copy.start()
-    for k in range(CHUNKS):
-        emb_copy(k).start(priority=0 if k < FIRST else 1)
+    for h in range(2):
+        basis_copy(h).start(priority=h)
+        for k in range(CHUNKS):
+            emb_copy(h, k).start(priority=h)
 
     cluster_copy.wait()
     index_copy.wait()
@@ -98,19 +107,22 @@
         here = jnp.where(cluster == c, rank.astype(jnp.float32), -1.0).astype(jnp.bfloat16)
         place[c * depth:(c + 1) * depth, :] = jnp.where(seat == here, one, none)
 
-    basis_copy.wait()
     size = 256
-    for k in range(n_rows // size):
-        if k * size == 0:
-            for q in range(FIRST):
-                emb_copy(q).wait()
-        if k * size == FIRST * step:
-            for q in range(FIRST, CHUNKS):
-                emb_copy(q).wait()
-        part = slice(k * size, (k + 1) * size)
-        projected = jnp.dot(emb[part, :], basis[...], preferred_element_type=jnp.float32)
-        scale = lax.rsqrt(jnp.sum(projected * projected, axis=1, keepdims=True) + 1e-06)
-        rows[part, :] = (projected * scale).astype(jnp.bfloat16)
+    for h in range(2):
+        basis_copy(h).wait()
+        for k in range(CHUNKS):
+            emb_copy(h, k).wait()
+        for k in range(n_rows // size):
+            part = slice(k * size, (k + 1) * size)
+            projected = jnp.dot(
+                emb[part, spans[h]], basis[spans[h], :], preferred_element_type=jnp.float32
+            )
+            if h == 0:
+                partial[part, :] = projected
+            else:
+                projected = projected + partial[part, :]
+                scale = lax.rsqrt(jnp.sum(projected * projected, axis=1, keepdims=True) + 1e-06)
+                rows[part, :] = (projected * scale).astype(jnp.bfloat16)
     tall = min(512, clusters * depth)
     per = tall // depth
     for t in range(clusters // per):
@@ -237,10 +249,11 @@
             pltpu.VMEM((1, doc_rows), jnp.int32),
             pltpu.VMEM((doc_rows, width), jnp.bfloat16),
             pltpu.VMEM((width, features), jnp.bfloat16),
+            pltpu.VMEM((doc_rows, features), jnp.float32),
             pltpu.VMEM((doc_rows, features), jnp.bfloat16),
             pltpu.VMEM((clusters * depth, doc_rows), jnp.bfloat16),
-            pltpu.SemaphoreType.DMA((CHUNKS,)),
-            pltpu.SemaphoreType.DMA,
+            pltpu.SemaphoreType.DMA((2, CHUNKS)),
+            pltpu.SemaphoreType.DMA((2,)),
             pltpu.SemaphoreType.DMA((2,)),
         ],
     )(*[pltpu.with_memory_space_constraint(a, pltpu.HBM) for a in (cluster_row, index_row, embeddings, pca_basis)])

time: 54.8 us -> 54.8 us (level)
  no operation moved by 1% of the time
where the time goes in v7:
time: 54.8 us; the launch traced here: 54.7 us
  blocking collectives  44.7 us (82%)
  Pallas kernels  9.93 us (18%)
    all_to_all x1, blocking collectives, on_device(): recv = lax.all_to_all(send, AXES, split_axis=0, concat_axis=0, tiled=True)  35.8 us
    all_to_all x1, blocking collectives, on_device(): back = lax.all_to_all(found, AXES, split_axis=0, concat_axis=0, tiled=True)  8.87 us
    pallas_call x1, Pallas kernels, on_device(): pl.pallas_call(pack, name='project_and_pack', compiler_params=pltpu.Compi...  6.86 us
    pallas_call x1, Pallas kernels, on_device(): pl.pallas_call(search, name='nearest', compiler_params=pltpu.CompilerPara...  2.2 us

profile of v7, /device:TPU:0, one launch (start us, length us, event | category | flops | bytes accessed | tf_op | source)
XLA Modules:
  0.0 54.7 jit_solution(4262351305491586008)
XLA Ops:
  0.0 6.9 %project_and_pack.1 = (bf16[32,33,4,128]{3,2,1,0:T(4,128)(2,1)S(1)}, s32[1,1024]{1,0:T(1,128)S(1)}) custom-call(s32[1,1024]{1,0:T(1,128)} %bitcast.3, s32[1,1024]{1,0:T(1,128)} %bitcast.5, bf16[1024,4096]{1,0:T(8,128)(2,1)} %refs_2_.1, bf16[4096,256]{1,0:T(8,128)(2,1)} %refs_3_.1), custom_call_target="tpu_custom_call" | custom-call | tf_op jit(solution)/shard_map/project_and_pack/pallas_call | solution.py:237
  6.9 0.0 copy-start
  6.9 35.8 %all_to_all.10.refs_0_ = bf16[32,33,4,128]{3,2,1,0:T(4,128)(2,1)S(1)} all-to-all(bf16[32,33,4,128]{3,2,1,0:T(4,128)(2,1)S(1)} %get-tuple-element.7), channel_id=1, replica_groups=mesh['docs'=8,'rep'=4] {'docs','rep'}, dimensions={0} | all-to-all | bytes 2162688 | tf_op jit(solution)/shard_map/all_to_all | solution.py:260
  42.7 2.2 %nearest.1 = f32[32,1,128]{2,1,0:T(1,128)S(1)} custom-call(bf16[32,33,4,128]{3,2,1,0:T(4,128)(2,1)S(1)} %all_to_all.10.refs_0_), custom_call_target="tpu_custom_call" | custom-call | tf_op jit(solution)/shard_map/nearest/pallas_call | solution.py:265
  44.9 8.9 %all_to_all.11.back_ref = f32[32,1,128]{2,1,0:T(1,128)S(1)} all-to-all(f32[32,1,128]{2,1,0:T(1,128)S(1)} %nearest.1), channel_id=1, replica_groups=mesh['docs'=8,'rep'=4] {'docs','rep'}, dimensions={0} | all-to-all | bytes 32768 | tf_op jit(solution)/shard_map/all_to_all | solution.py:278
  53.8 0.0 copy-done
  53.8 0.9 %collect.1 = f32[1,1024]{1,0:T(1,128)} custom-call(f32[32,1,128]{2,1,0:T(1,128)S(1)} %all_to_all.11.back_ref, s32[1,1024]{1,0:T(1,128)S(1)} %bitcast.4, s32[1,1024]{1,0:T(1,128)S(1)} %get-tuple-element.8.lane_ref), custom_call_target="tpu_custom_call" | custom-call | tf_op jit(solution)/shard_map/collect/pallas_call | solution.py:279
Async XLA Ops:
  6.9 46.9 %copy-start = (s32[1024,1]{0,1:T(1,128)S(1)}, s32[1024,1]{0,1:T(1,128)}, u32[]{:S(2)}) copy-start(s32[1024,1]{0,1:T(1,128)} %param.6) | copy-start | bytes 12292

commit v8 on v7

--- a/solution.py
+++ b/solution.py
@@ -160,20 +160,21 @@
         col[c * depth:(c + 1) * depth, :] = jnp.broadcast_to(
             turned[:depth, c:c + 1], (depth, LANES)
         )
-    tile = 256
+    tile = 512
     tiles = slots // tile
+    halves = tile // LANES
     tops = {}
     for i in range(tiles):
         right = x[i * tile:(i + 1) * tile, :]
-        best = [jnp.full((8, LANES), -1.0, jnp.float32) for _ in range(2)]
+        best = [jnp.full((8, LANES), -1.0, jnp.float32) for _ in range(halves)]
         for j in range(i + 1):
             scores = nt_dot(x[j * tile:(j + 1) * tile, :], right)
             part = slice(j * tile, (j + 1) * tile)
             here = col[part, :]
             mirrored = None
-            for h in range(2):
+            for h in range(halves):
                 mine = scores[:, h * LANES:(h + 1) * LANES]
-                before = here > rows_of[2 * i + h]
+                before = here > rows_of[halves * i + h]
                 kept = jnp.where(before, mine, -1.0)
                 best[h] = jnp.maximum(best[h], jnp.max(kept.reshape(tile // 8, 8, LANES), axis=0))
                 if j < i:
@@ -185,13 +186,13 @@
                 if i < tiles - 1:
                     side[part, :] = mirrored
                 else:
-                    for h in range(2):
+                    for h in range(halves):
                         turned_side = mirrored[h * LANES:(h + 1) * LANES, :].T
-                        tops[2 * j + h] = jnp.maximum(
-                            tops[2 * j + h], jnp.max(turned_side, axis=0, keepdims=True)
+                        tops[halves * j + h] = jnp.maximum(
+                            tops[halves * j + h], jnp.max(turned_side, axis=0, keepdims=True)
                         )
-        for h in range(2):
-            tops[2 * i + h] = jnp.max(best[h], axis=0, keepdims=True)
+        for h in range(halves):
+            tops[halves * i + h] = jnp.max(best[h], axis=0, keepdims=True)
     for k in range(slots // LANES):
         for q in range(group):
             out_ref[k * group + q] = tops[k]

time: 54.8 us -> 54.7 us (level)
  no operation moved by 1% of the time
where the time goes in v8:
time: 54.7 us; the launch traced here: 54.6 us
  blocking collectives  44.7 us (82%)
  Pallas kernels  9.85 us (18%)
    all_to_all x1, blocking collectives, on_device(): recv = lax.all_to_all(send, AXES, split_axis=0, concat_axis=0, tiled=True)  35.8 us
    all_to_all x1, blocking collectives, on_device(): back = lax.all_to_all(found, AXES, split_axis=0, concat_axis=0, tiled=True)  8.87 us
    pallas_call x1, Pallas kernels, on_device(): pl.pallas_call(pack, name='project_and_pack', compiler_params=pltpu.Compi...  6.86 us
    pallas_call x1, Pallas kernels, on_device(): pl.pallas_call(search, name='nearest', compiler_params=pltpu.CompilerPara...  2.12 us

profile of v8, /device:TPU:0, one launch (start us, length us, event | category | flops | bytes accessed | tf_op | source)
XLA Modules:
  0.0 54.6 jit_solution(1190438662387499575)
XLA Ops:
  0.0 6.9 %project_and_pack.1 = (bf16[32,33,4,128]{3,2,1,0:T(4,128)(2,1)S(1)}, s32[1,1024]{1,0:T(1,128)S(1)}) custom-call(s32[1,1024]{1,0:T(1,128)} %bitcast.3, s32[1,1024]{1,0:T(1,128)} %bitcast.5, bf16[1024,4096]{1,0:T(8,128)(2,1)} %refs_2_.1, bf16[4096,256]{1,0:T(8,128)(2,1)} %refs_3_.1), custom_call_target="tpu_custom_call" | custom-call | tf_op jit(solution)/shard_map/project_and_pack/pallas_call | solution.py:238
  6.9 0.0 copy-start
  6.9 35.8 %all_to_all.10.refs_0_ = bf16[32,33,4,128]{3,2,1,0:T(4,128)(2,1)S(1)} all-to-all(bf16[32,33,4,128]{3,2,1,0:T(4,128)(2,1)S(1)} %get-tuple-element.7), channel_id=1, replica_groups=mesh['docs'=8,'rep'=4] {'docs','rep'}, dimensions={0} | all-to-all | bytes 2162688 | tf_op jit(solution)/shard_map/all_to_all | solution.py:261
  42.7 2.1 %nearest.1 = f32[32,1,128]{2,1,0:T(1,128)S(1)} custom-call(bf16[32,33,4,128]{3,2,1,0:T(4,128)(2,1)S(1)} %all_to_all.10.refs_0_), custom_call_target="tpu_custom_call" | custom-call | tf_op jit(solution)/shard_map/nearest/pallas_call | solution.py:266
  44.8 8.9 %all_to_all.11.back_ref = f32[32,1,128]{2,1,0:T(1,128)S(1)} all-to-all(f32[32,1,128]{2,1,0:T(1,128)S(1)} %nearest.1), channel_id=1, replica_groups=mesh['docs'=8,'rep'=4] {'docs','rep'}, dimensions={0} | all-to-all | bytes 32768 | tf_op jit(solution)/shard_map/all_to_all | solution.py:279
  53.7 0.0 copy-done
  53.7 0.9 %collect.1 = f32[1,1024]{1,0:T(1,128)} custom-call(f32[32,1,128]{2,1,0:T(1,128)S(1)} %all_to_all.11.back_ref, s32[1,1024]{1,0:T(1,128)S(1)} %bitcast.4, s32[1,1024]{1,0:T(1,128)S(1)} %get-tuple-element.8.lane_ref), custom_call_target="tpu_custom_call" | custom-call | tf_op jit(solution)/shard_map/collect/pallas_call | solution.py:280
Async XLA Ops:
  6.9 46.8 %copy-start = (s32[1024,1]{0,1:T(1,128)S(1)}, s32[1024,1]{0,1:T(1,128)}, u32[]{:S(2)}) copy-start(s32[1024,1]{0,1:T(1,128)} %param.6) | copy-start | bytes 12292

commit v9 on v7

--- a/solution.py
+++ b/solution.py
@@ -7,6 +7,7 @@
 
 CL_DEV = 4
 AXES = ("docs", "rep")
+OWNERS = ("rep", "docs")
 LANES = 128
 ROWS = 4
 CHUNKS = 2
@@ -79,7 +80,7 @@
         ranks.append(jnp.sum(mine * (part[:, :LANES] + carry), axis=0, keepdims=True))
         carry = carry + part[:, LANES:]
     rank = jnp.concatenate(ranks, axis=1).astype(jnp.int32)
-    me = lax.axis_index("docs") * lax.axis_size("rep") + lax.axis_index("rep")
+    me = lax.axis_index("rep") * lax.axis_size("docs") + lax.axis_index("docs")
     lane_ref[...] = rank + (me % (LANES // depth)) * depth
 
     rank_hot = (
@@ -257,7 +258,7 @@
             pltpu.SemaphoreType.DMA((2,)),
         ],
     )(*[pltpu.with_memory_space_constraint(a, pltpu.HBM) for a in (cluster_row, index_row, embeddings, pca_basis)])
-    recv = lax.all_to_all(send, AXES, split_axis=0, concat_axis=0, tiled=True)
+    recv = lax.all_to_all(send, OWNERS, split_axis=0, concat_axis=0, tiled=True)
 
     def search(*refs):
         nearest_kernel(*refs, depth=depth)
@@ -275,7 +276,7 @@
             pltpu.VMEM((n_dev * depth, LANES), jnp.float32),
         ],
     )(recv)
-    back = lax.all_to_all(found, AXES, split_axis=0, concat_axis=0, tiled=True)
+    back = lax.all_to_all(found, OWNERS, split_axis=0, concat_axis=0, tiled=True)
     nearest = pl.pallas_call(
         collect_kernel,
         name="collect",

time: 54.8 us -> 54.7 us (level)
  no operation moved by 1% of the time
where the time goes in v9:
time: 54.7 us; the launch traced here: 54.6 us
  blocking collectives  44.6 us (82%)
  Pallas kernels  9.92 us (18%)
    all_to_all x1, blocking collectives, on_device(): recv = lax.all_to_all(send, OWNERS, split_axis=0, concat_axis=0, tiled=True)  35.7 us
    all_to_all x1, blocking collectives, on_device(): lax.all_to_all(found, OWNERS, split_axis=0, concat_axis=0, tiled=True)  8.89 us
    pallas_call x1, Pallas kernels, on_device(): pl.pallas_call(pack, name='project_and_pack', compiler_params=pltpu.Compi...  6.86 us
    pallas_call x1, Pallas kernels, on_device(): pl.pallas_call(search, name='nearest', compiler_params=pltpu.CompilerPara...  2.2 us

profile of v9, /device:TPU:0, one launch (start us, length us, event | category | flops | bytes accessed | tf_op | source)
XLA Modules:
  0.0 54.6 jit_solution(9277518411859337232)
XLA Ops:
  0.0 6.9 %project_and_pack.1 = (bf16[32,33,4,128]{3,2,1,0:T(4,128)(2,1)S(1)}, s32[1,1024]{1,0:T(1,128)S(1)}) custom-call(s32[1,1024]{1,0:T(1,128)} %bitcast.3, s32[1,1024]{1,0:T(1,128)} %bitcast.5, bf16[1024,4096]{1,0:T(8,128)(2,1)} %refs_2_.1, bf16[4096,256]{1,0:T(8,128)(2,1)} %refs_3_.1), custom_call_target="tpu_custom_call" | custom-call | tf_op jit(solution)/shard_map/project_and_pack/pallas_call | solution.py:238
  6.9 0.0 copy-start
  6.9 35.7 %all_to_all.10.refs_0_ = bf16[32,33,4,128]{3,2,1,0:T(4,128)(2,1)S(1)} all-to-all(bf16[32,33,4,128]{3,2,1,0:T(4,128)(2,1)S(1)} %get-tuple-element.7), channel_id=1, replica_groups=mesh['docs'=8,'rep'=4] {'rep','docs'}, dimensions={0} | all-to-all | bytes 2162688 | tf_op jit(solution)/shard_map/all_to_all | solution.py:261
  42.6 2.2 %nearest.1 = f32[32,1,128]{2,1,0:T(1,128)S(1)} custom-call(bf16[32,33,4,128]{3,2,1,0:T(4,128)(2,1)S(1)} %all_to_all.10.refs_0_), custom_call_target="tpu_custom_call" | custom-call | tf_op jit(solution)/shard_map/nearest/pallas_call | solution.py:266
  44.8 8.9 %all_to_all.11.back_ref = f32[32,1,128]{2,1,0:T(1,128)S(1)} all-to-all(f32[32,1,128]{2,1,0:T(1,128)S(1)} %nearest.1), channel_id=1, replica_groups=mesh['docs'=8,'rep'=4] {'rep','docs'}, dimensions={0} | all-to-all | bytes 32768 | tf_op jit(solution)/shard_map/all_to_all | solution.py:279
  53.7 0.0 copy-done
  53.7 0.9 %collect.1 = f32[1,1024]{1,0:T(1,128)} custom-call(f32[32,1,128]{2,1,0:T(1,128)S(1)} %all_to_all.11.back_ref, s32[1,1024]{1,0:T(1,128)S(1)} %bitcast.4, s32[1,1024]{1,0:T(1,128)S(1)} %get-tuple-element.8.lane_ref), custom_call_target="tpu_custom_call" | custom-call | tf_op jit(solution)/shard_map/collect/pallas_call | solution.py:280
Async XLA Ops:
  6.9 46.8 %copy-start = (s32[1024,1]{0,1:T(1,128)S(1)}, s32[1024,1]{0,1:T(1,128)}, u32[]{:S(2)}) copy-start(s32[1024,1]{0,1:T(1,128)} %param.6) | copy-start | bytes 12292
